TPU v7x, 512 devices: a 8x2x16 block of a 8x8x16 slice. The times are simulated.
512 devices in a mesh: groups: 2 (over y), mp: 16 (over z), dp: 8 (over x), guide: 2 (over core).
Axes of the slice: x: 8, y: 2, z: 16, core: 2. Of those that a mesh axis runs over, the one named last changes fastest.
The devices are a block of a 8x8x16 slice.
Arguments:
- tokens: bfloat16 [768, 8192], P(('groups', 'mp'), ('dp', 'guide')), parts along dimension 0, may hold values from -6 to 6
- w_gate: bfloat16 [8192, 14336], P(('dp', 'guide'), 'mp'), may hold values from -0.0625 to 0.0625
- w_up: bfloat16 [8192, 14336], P(('dp', 'guide'), 'mp'), may hold values from -0.0625 to 0.0625
- w_down: bfloat16 [14336, 8192], P('mp', ('dp', 'guide')), may hold values from -0.046875 to 0.046875
Outputs:
- layer_output: bfloat16 [768, 8192], P(('groups', 'mp'), ('dp', 'guide')), parts along dimension 0
There are 2 independent parts, one for each index of `groups`. A program takes and returns all parts, laid end to end along the dimension named above; an argument that names none is the same for every part. Nothing has to cross between parts.
All inputs are finite; a program needn't handle non-finite values.
Results may differ from a plain program's by a relative error of at most 0.0049.
Values may be sent and summed in bfloat16 or wider, within the bound.
No kernel may reach another device: no remote copies, remote signals or barrier semaphores. Data moves between devices by JAX's collectives and lax.ppermute only.
A program may use at most 64 MiB of HBM per device.

v0:
```python
import jax
import jax.numpy as jnp
from jax import lax
from jax.sharding import PartitionSpec as P


def copy_for_each(shard, axis):
    count = lax.axis_size(axis)
    return lax.all_to_all(
        jnp.broadcast_to(shard[None], (count, *shard.shape)), axis, 0, 0, tiled=True
    )


def laid_out(tiles, dim):
    tiles = jnp.moveaxis(tiles, 0, dim)
    shape = tiles.shape
    return tiles.reshape(*shape[:dim], shape[dim] * shape[dim + 1], *shape[dim + 2 :])


def gathered_copies(shard, axis, dim):
    tiles = copy_for_each(shard, axis)
    return laid_out(tiles, dim)


def cut_along(shard, dim, count):
    before, after = (shard.shape[:dim], shard.shape[dim + 1 :])
    return jnp.moveaxis(shard.reshape(*before, count, -1, *after), dim, 0)


def summed_on_arrival(shard, axis, dim):
    tiles = cut_along(shard, dim, lax.axis_size(axis))
    arrived = lax.all_to_all(tiles, axis, split_axis=0, concat_axis=0, tiled=True)
    return arrived.sum(axis=0)


def per_device(tokens, w_gate, w_up, w_down):
    columns = w_gate.shape[1]
    paired_weights = jnp.concatenate([w_gate, w_up], axis=1)
    partial_terms = jnp.dot(
        gathered_copies(tokens, "mp", 0), paired_weights, preferred_element_type=jnp.float32
    )
    summed = summed_on_arrival(partial_terms, ("dp", "guide"), 0)
    hidden_share = (jax.nn.silu(summed[:, :columns]) * summed[:, columns:]).astype(jnp.bfloat16)
    hidden = lax.all_gather(hidden_share, ("dp", "guide"), axis=0, tiled=True)
    output_share = summed_on_arrival(
        jnp.dot(hidden, w_down, preferred_element_type=jnp.float32), "mp", 0
    )
    return output_share.astype(jnp.bfloat16)


def solution(mesh):
    placed = (
        P(("groups", "mp"), ("dp", "guide")),
        P(("dp", "guide"), "mp"),
        P(("dp", "guide"), "mp"),
        P("mp", ("dp", "guide")),
    )
    return jax.shard_map(
        per_device,
        mesh=mesh,
        in_specs=placed,
        out_specs=P(("groups", "mp"), ("dp", "guide")),
        check_vma=False,
    )
```

profile of v0, /device:TPU:80, one launch (start us, length us, event | category | flops | bytes accessed | tf_op | source)
XLA Modules:
  0.0 210.1 jit_solution(8192916604635931104)
XLA Ops:
  0.0 0.0 copy-start
  0.0 0.8 broadcast_in_dim.2
  0.9 67.2 %all_to_all.15 = bf16[16,24,512]{2,1,0:T(8,128)(2,1)S(1)} all-to-all(bf16[16,24,512]{2,1,0:T(8,128)(2,1)S(1)} %broadcast_in_dim.2), channel_id=1, replica_groups=mesh['groups'=2,'mp'=16,'dp'=8,'guide'=2] {'mp'}, dimensions={0} | all-to-all | bytes 786432 | tf_op jit(solution)/shard_map/all_to_all | solution.py:9
  68.1 2.3 %fusion = f32[1792,384]{0,1:T(8,128)S(1)} fusion(bf16[384,512]{1,0:T(8,128)(2,1)S(1)} %bitcast.10, bf16[512,896]{1,0:T(8,128)(2,1)} %param.6, bf16[512,896]{1,0:T(8,128)(2,1)} %param.5), kind=kOutput, calls=%fused_computation | convolution fusion | flops 708313088 | bytes 4980736 | tf_op jit(solution)/shard_map/dot_general | solution.py:39
  70.4 72.2 %all_to_all.16 = f32[16,24,1792]{2,1,0:T(8,128)} all-to-all(f32[16,24,1792]{2,1,0:T(8,128)S(1)} %bitcast.8), channel_id=1, replica_groups=mesh['groups'=2,'mp'=16,'dp'=8,'guide'=2] {'dp','guide'}, dimensions={0} | all-to-all | bytes 5505024 | tf_op jit(solution)/shard_map/all_to_all | solution.py:32
  142.6 1.9 reduce_sum.18
  144.6 16.8 %all_gather.3 = bf16[384,896]{1,0:T(8,128)(2,1)S(1)} all-gather(bf16[24,896]{1,0:T(8,128)(2,1)S(1)} %fusion.4), channel_id=1, replica_groups=mesh['groups'=2,'mp'=16,'dp'=8,'guide'=2] {'dp','guide'}, dimensions={0}, use_global_device_ids=true | all-gather | bytes 731136 | tf_op jit(solution)/shard_map/all_gather | solution.py:44
  161.4 0.0 copy-done
  161.4 0.6 fusion.6
  162.0 47.5 %all_to_all.17 = f32[16,24,512]{2,1,0:T(8,128)S(1)} all-to-all(f32[16,24,512]{2,1,0:T(8,128)S(1)} %bitcast.9), channel_id=1, replica_groups=mesh['groups'=2,'mp'=16,'dp'=8,'guide'=2] {'mp'}, dimensions={0} | all-to-all | bytes 1572864 | tf_op jit(solution)/shard_map/all_to_all | solution.py:32
  209.4 0.7 reduce_sum.19
  (1 shorter events, 0.0 us)
Async XLA Ops:
  0.0 161.4 %copy-start = (bf16[896,512]{1,0:T(8,128)(2,1)S(1)}, bf16[896,512]{1,0:T(8,128)(2,1)}, u32[]{:S(2)}) copy-start(bf16[896,512]{1,0:T(8,128)(2,1)} %param.7) | copy-start | bytes 2752516
where the time goes:
time: 210 us
  blocking collectives  204 us (97%)
  matrix products  2.9 us (1%)
  other arithmetic  2.62 us (1%)
    all_to_all x2, blocking collectives, summed_on_arrival(): lax.all_to_all(tiles, axis, split_axis=0, concat_axis=0, tiled=True)  120 us
    all_to_all x1, blocking collectives, copy_for_each(): lax.all_to_all(jnp.broadcast_to(shard[None], (count, *shard.shape)), axis...  67.2 us
    all_gather x1, blocking collectives, per_device(): hidden = lax.all_gather(hidden_share, ('dp', 'guide'), axis=0, tiled=True)  16.8 us

commit v1 on v0

v1 whole, which is shorter than its diff:
```python
import jax
import jax.numpy as jnp
from jax import lax
from jax.sharding import PartitionSpec as P


def summed_on_arrival(tiles, axis):
    arrived = lax.all_to_all(tiles, axis, split_axis=0, concat_axis=0, tiled=True)
    return arrived.astype(jnp.float32).sum(axis=0)


def cut(shard, count):
    return shard.reshape(count, shard.shape[0] // count, *shard.shape[1:])


def per_device(tokens, w_gate, w_up, w_down):
    columns = w_gate.shape[1]
    mp, dp, guide = (lax.axis_size(axis) for axis in ("mp", "dp", "guide"))
    paired_weights = jnp.concatenate([w_gate, w_up], axis=1)
    blocks = lax.all_gather(tokens, "mp", axis=0, tiled=False)
    blocks = blocks.reshape(dp, guide, -1, *tokens.shape)
    gathered = blocks.swapaxes(0, 1).reshape(-1, tokens.shape[1])
    partial_terms = jnp.dot(gathered, paired_weights, preferred_element_type=jnp.float32)
    chip_terms = summed_on_arrival(cut(partial_terms, guide), "guide").astype(jnp.bfloat16)
    summed = summed_on_arrival(cut(chip_terms, dp), "dp")
    hidden_share = (jax.nn.silu(summed[:, :columns]) * summed[:, columns:]).astype(jnp.bfloat16)
    hidden = lax.all_gather(hidden_share, ("dp", "guide"), axis=0, tiled=True)
    output_terms = jnp.dot(hidden, w_down, preferred_element_type=jnp.float32).astype(jnp.bfloat16)
    return summed_on_arrival(cut(output_terms, mp), "mp").astype(jnp.bfloat16)


def solution(mesh):
    placed = (
        P(("groups", "mp"), ("dp", "guide")),
        P(("dp", "guide"), "mp"),
        P(("dp", "guide"), "mp"),
        P("mp", ("dp", "guide")),
    )
    return jax.shard_map(
        per_device,
        mesh=mesh,
        in_specs=placed,
        out_specs=P(("groups", "mp"), ("dp", "guide")),
        check_vma=False,
    )
```

time: 210 us -> 156 us (0.74)
  blocking collectives: 204 us -> 150 us
    all_gather x0 -> x1, blocking collectives: none -> 70.5 us  [per_device(): blocks = lax.all_gather(tokens, 'mp', axis=0, tiled=False)]
    all_to_all x1 -> x0, blocking collectives: 67.2 us -> none  [copy_for_each(): lax.all_to_all(jnp.broadcast_to(shard[None], (count, *shard.shape)), axis...]
    all_to_all x2 -> x3, blocking collectives: 120 us -> 62.6 us  [summed_on_arrival(): lax.all_to_all(tiles, axis, split_axis=0, concat_axis=0, tiled=True)]
where the time goes in v1:
time: 156 us
  blocking collectives  150 us (96%)
  matrix products  2.91 us (2%)
  other arithmetic  2.8 us (2%)
    all_gather x1, blocking collectives, per_device(): blocks = lax.all_gather(tokens, 'mp', axis=0, tiled=False)  70.5 us
    all_to_all x3, blocking collectives, summed_on_arrival(): lax.all_to_all(tiles, axis, split_axis=0, concat_axis=0, tiled=True)  62.6 us
    all_gather x1, blocking collectives, per_device(): hidden = lax.all_gather(hidden_share, ('dp', 'guide'), axis=0, tiled=True)  16.6 us

profile of v1, /device:TPU:80, one launch (start us, length us, event | category | flops | bytes accessed | tf_op | source)
XLA Modules:
  0.0 155.5 jit_solution(7631162222626804880)
XLA Ops:
  0.0 0.0 copy-start
  0.0 70.5 %all-gather = bf16[384,512]{1,0:T(8,128)(2,1)S(1)} all-gather(bf16[24,512]{1,0:T(8,128)(2,1)} %param.4), channel_id=2, replica_groups=mesh['groups'=2,'mp'=16,'dp'=8,'guide'=2] {'mp'}, dimensions={0}, use_global_device_ids=true | all-gather | bytes 417792 | tf_op jit(solution)/shard_map/all_gather | solution.py:20
  70.6 2.3 %fusion = f32[1792,384]{0,1:T(8,128)S(1)} fusion(bf16[384,512]{1,0:T(8,128)(2,1)S(1)} %bitcast.14, bf16[512,896]{1,0:T(8,128)(2,1)} %param.6, bf16[512,896]{1,0:T(8,128)(2,1)} %param.5), kind=kOutput, calls=%fused_computation | convolution fusion | flops 708313088 | bytes 4980736 | tf_op jit(solution)/shard_map/dot_general | solution.py:23
  72.9 6.9 %all_to_all.15 = f32[2,192,1792]{2,1,0:T(8,128)} all-to-all(f32[2,192,1792]{2,1,0:T(8,128)S(1)} %bitcast.12), channel_id=1, replica_groups=mesh['groups'=2,'mp'=16,'dp'=8,'guide'=2] {'guide'}, dimensions={0} | all-to-all | bytes 5505024 | tf_op jit(solution)/shard_map/all_to_all | solution.py:8
  79.8 2.0 %reduce_sum.30 = bf16[192,1792]{1,0:T(8,128)(2,1)S(1)} reduce(f32[2,192,1792]{2,1,0:T(8,128)} %all_to_all.15, f32[]{:T(128)} %constant.4.clone.1), dimensions={0}, to_apply=%region_0.0 | reduce | flops 344064 | bytes 3440644 | tf_op jit(solution)/shard_map/reduce_sum | solution.py:9
  81.8 28.4 %all_to_all.16 = bf16[8,24,1792]{2,1,0:T(8,128)(2,1)S(1)} all-to-all(bf16[8,24,1792]{2,1,0:T(8,128)(2,1)S(1)} %bitcast.13), channel_id=1, replica_groups=mesh['groups'=2,'mp'=16,'dp'=8,'guide'=2] {'dp'}, dimensions={0} | all-to-all | bytes 1376256 | tf_op jit(solution)/shard_map/all_to_all | solution.py:8
  110.2 0.1 convert_reduce_fusion
  110.4 16.6 %all_gather.11 = bf16[384,896]{1,0:T(8,128)(2,1)S(1)} all-gather(bf16[24,896]{1,0:T(8,128)(2,1)S(1)} %fusion.4), channel_id=1, replica_groups=mesh['groups'=2,'mp'=16,'dp'=8,'guide'=2] {'dp','guide'}, dimensions={0}, use_global_device_ids=true | all-gather | bytes 731136 | tf_op jit(solution)/shard_map/all_gather | solution.py:27
  127.0 0.0 copy-done
  127.0 0.6 convolution_convert_fusion
  127.6 27.3 %all_to_all.17 = bf16[16,24,512]{2,1,0:T(8,128)(2,1)S(1)} all-to-all(bf16[16,24,512]{2,1,0:T(8,128)(2,1)S(1)} %bitcast.16), channel_id=1, replica_groups=mesh['groups'=2,'mp'=16,'dp'=8,'guide'=2] {'mp'}, dimensions={0} | all-to-all | bytes 786432 | tf_op jit(solution)/shard_map/all_to_all | solution.py:8
  154.9 0.7 reduce_sum.32
  (2 shorter events, 0.1 us)
Async XLA Ops:
  0.0 127.0 %copy-start = (bf16[896,512]{1,0:T(8,128)(2,1)S(1)}, bf16[896,512]{1,0:T(8,128)(2,1)}, u32[]{:S(2)}) copy-start(bf16[896,512]{1,0:T(8,128)(2,1)} %param.7) | copy-start | bytes 2752516

commit v2 on v1

v2 whole, which is shorter than its diff:
```python
import jax
import jax.numpy as jnp
from jax import lax
from jax.sharding import PartitionSpec as P


def summed_on_arrival(tiles, axis):
    arrived = lax.all_to_all(tiles, axis, split_axis=0, concat_axis=0, tiled=True)
    total = arrived[0].astype(jnp.float32)
    for tile in arrived[1:]:
        total = total + tile.astype(jnp.float32)
    return total


def from_other_core(array):
    count = lax.axis_size("guide")
    return lax.ppermute(array, "guide", [(core, (core + 1) % count) for core in range(count)])


def per_device(tokens, w_gate, w_up, w_down):
    columns = w_gate.shape[1]
    rows, features = tokens.shape
    mp, dp, guide = (lax.axis_size(axis) for axis in ("mp", "dp", "guide"))
    core = lax.axis_index("guide")
    own_weights = jnp.concatenate([w_gate, w_up], axis=1)
    other_weights = jnp.concatenate([from_other_core(w_gate), from_other_core(w_up)], axis=1)
    blocks = lax.all_gather(tokens, ("mp", "guide"), axis=0, tiled=False)
    blocks = blocks.reshape(dp, guide, guide, rows, features)
    mine = lax.dynamic_index_in_dim(blocks, core, 1, keepdims=False)
    own = lax.dynamic_index_in_dim(mine, core, 1, keepdims=False).reshape(-1, features)
    other = lax.dynamic_index_in_dim(mine, 1 - core, 1, keepdims=False).reshape(-1, features)
    chip_terms = jnp.dot(own, own_weights, preferred_element_type=jnp.float32) + jnp.dot(
        other, other_weights, preferred_element_type=jnp.float32
    )
    chip_terms = chip_terms.astype(jnp.bfloat16).reshape(dp, rows, -1)
    summed = summed_on_arrival(chip_terms, "dp")
    hidden_share = (jax.nn.silu(summed[:, :columns]) * summed[:, columns:]).astype(jnp.bfloat16)
    hidden = lax.all_gather(hidden_share, ("dp", "guide"), axis=0, tiled=True)
    output_terms = jnp.dot(hidden, w_down, preferred_element_type=jnp.float32).astype(jnp.bfloat16)
    return summed_on_arrival(output_terms.reshape(mp, rows, -1), "mp").astype(jnp.bfloat16)


def solution(mesh):
    placed = (
        P(("groups", "mp"), ("dp", "guide")),
        P(("dp", "guide"), "mp"),
        P(("dp", "guide"), "mp"),
        P("mp", ("dp", "guide")),
    )
    return jax.shard_map(
        per_device,
        mesh=mesh,
        in_specs=placed,
        out_specs=P(("groups", "mp"), ("dp", "guide")),
        check_vma=False,
    )
```

time: 156 us -> 154 us (0.987)
  blocking collectives: 150 us -> 144 us
  starting transfers between devices: 0 us -> 4.51 us
  other arithmetic: 2.8 us -> 0.79 us
    all_to_all x3 -> x2, blocking collectives: 62.6 us -> 55.9 us  [summed_on_arrival(): lax.all_to_all(tiles, axis, split_axis=0, concat_axis=0, tiled=True)]
    ppermute x0 -> x2, starting transfers between devices: none -> 4.51 us  [from_other_core(): lax.ppermute(array, 'guide', [(core, (core + 1) % count) for core in rang...]
    reduce_sum x3 -> x0, other arithmetic: 2.77 us -> none  [summed_on_arrival(): return arrived.astype(jnp.float32).sum(axis=0)]
    dot_general x1 -> x2, matrix products: 2.34 us -> 3.42 us  [the longest x1 1.71 us: per_device(): jnp.dot(other, other_weights, preferred_element_type=jnp.float32)]
  transfers between devices with their start and end apart: 0 -> 2, of which waited for: 0 -> 0; matrix products, arithmetic and copies ran while one was open for 0% -> 1% of each run, Pallas kernels for 0% -> 0%
where the time goes in v2:
time: 154 us; the launch traced here: 153 us
  blocking collectives  144 us (94%)
  starting transfers between devices  4.51 us (3%)
  matrix products  3.99 us (3%)
    all_gather x1, blocking collectives, per_device(): blocks = lax.all_gather(tokens, ('mp', 'guide'), axis=0, tiled=False)  71.3 us
    all_to_all x2, blocking collectives, summed_on_arrival(): lax.all_to_all(tiles, axis, split_axis=0, concat_axis=0, tiled=True)  55.9 us
    all_gather x1, blocking collectives, per_device(): hidden = lax.all_gather(hidden_share, ('dp', 'guide'), axis=0, tiled=True)  16.6 us
    ppermute x2, starting transfers between devices, from_other_core(): lax.ppermute(array, 'guide', [(core, (core + 1) % count) for core in rang...  4.51 us
  transfers between devices with their start and end apart: 2, of which 0 were waited for; matrix products, arithmetic and copies ran while one was open for 1% of the time, Pallas kernels for 0%

profile of v2, /device:TPU:80, one launch (start us, length us, event | category | flops | bytes accessed | tf_op | source)
XLA Modules:
  0.0 153.3 jit_solution(6196211997722715402)
XLA Ops:
  0.0 0.0 copy-start
  0.0 0.0 copy-start.1
  0.0 2.1 %collective-permute-start = (bf16[512,896]{1,0:T(8,128)(2,1)}, bf16[512,896]{1,0:T(8,128)(2,1)S(1)}, u32[]{:S(2)}, u32[]{:S(2)}) collective-permute-start(bf16[512,896]{1,0:T(8,128)(2,1)} %param.5), channel_id=1, source_target_pairs={{0,1},{1,0},{2,3},{3,2},{4,5},{5,4},{6,7},{7,6},{8,9},{9,8},{10,11... | collective-permute-start | bytes 2752520 | tf_op jit(solution)/shard_map/ppermute | solution.py:17
  2.1 2.4 %collective-permute-start.1 = (bf16[512,896]{1,0:T(8,128)(2,1)}, bf16[512,896]{1,0:T(8,128)(2,1)}, u32[]{:S(2)}, u32[]{:S(2)}) collective-permute-start(bf16[512,896]{1,0:T(8,128)(2,1)} %param.6), channel_id=1, source_target_pairs={{0,1},{1,0},{2,3},{3,2},{4,5},{5,4},{6,7},{7,6},{8,9},{9,8},{10,11... | collective-permute-start | bytes 2752520 | tf_op jit(solution)/shard_map/ppermute | solution.py:17
  4.5 71.3 %all-gather = bf16[768,512]{1,0:T(8,128)(2,1)S(1)} all-gather(bf16[24,512]{1,0:T(8,128)(2,1)} %param.4), channel_id=2, replica_groups=mesh['groups'=2,'mp'=16,'dp'=8,'guide'=2] {'mp','guide'}, dimensions={0}, use_global_device_ids=true | all-gather | bytes 811008 | tf_op jit(solution)/shard_map/all_gather | solution.py:27
  75.9 0.0 copy-done.1
  75.9 1.7 %fusion.1 = f32[192,1792]{1,0:T(8,128)S(1)} fusion(bf16[192,512]{1,0:T(8,128)(2,1)S(1)} %bitcast.22, bf16[512,896]{1,0:T(8,128)(2,1)} %param.6, bf16[512,896]{1,0:T(8,128)(2,1)S(1)} %copy-done.1), kind=kOutput, calls=%fused_computation.2 | convolution fusion | flops 355991552 | bytes 3407872 | tf_op jit(solution)/shard_map/dot_general | solution.py:32
  77.6 0.0 collective-permute-done
  77.6 0.0 collective-permute-done.1
  77.6 1.7 %fusion = bf16[192,1792]{1,0:T(8,128)(2,1)S(1)} fusion(f32[192,1792]{1,0:T(8,128)S(1)} %fusion.1, bf16[192,512]{1,0:T(8,128)(2,1)S(1)} %bitcast.21, bf16[512,896]{1,0:T(8,128)(2,1)} %collective-permute-done.1, bf16[512,896]{1,0:T(8,128)(2,1)S(1)} %collective-permute-done), kind=kOutput, calls=%fused_computation.1 | convolution fusion | flops 356679680 | bytes 4096000 | tf_op jit(solution)/shard_map/dot_general | solution.py:32
  79.3 28.6 %all_to_all.10 = bf16[8,24,1792]{2,1,0:T(8,128)(2,1)S(1)} all-to-all(bf16[8,24,1792]{2,1,0:T(8,128)(2,1)S(1)} %bitcast.19), channel_id=1, replica_groups=mesh['groups'=2,'mp'=16,'dp'=8,'guide'=2] {'dp'}, dimensions={0} | all-to-all | bytes 1376256 | tf_op jit(solution)/shard_map/all_to_all | solution.py:8
  108.0 0.1 add_bitcast_fusion
  108.1 16.6 %all_gather.11 = bf16[384,896]{1,0:T(8,128)(2,1)S(1)} all-gather(bf16[24,896]{1,0:T(8,128)(2,1)S(1)} %fusion.8), channel_id=1, replica_groups=mesh['groups'=2,'mp'=16,'dp'=8,'guide'=2] {'dp','guide'}, dimensions={0}, use_global_device_ids=true | all-gather | bytes 731136 | tf_op jit(solution)/shard_map/all_gather | solution.py:38
  124.7 0.0 copy-done
  124.7 0.6 convolution_convert_fusion
  125.3 27.3 %all_to_all.11 = bf16[16,24,512]{2,1,0:T(8,128)(2,1)S(1)} all-to-all(bf16[16,24,512]{2,1,0:T(8,128)(2,1)S(1)} %bitcast.20), channel_id=1, replica_groups=mesh['groups'=2,'mp'=16,'dp'=8,'guide'=2] {'mp'}, dimensions={0} | all-to-all | bytes 786432 | tf_op jit(solution)/shard_map/all_to_all | solution.py:8
  152.6 0.7 fusion.9
  (2 shorter events, 0.1 us)
Async XLA Ops:
  0.0 124.7 %copy-start = (bf16[896,512]{1,0:T(8,128)(2,1)S(1)}, bf16[896,512]{1,0:T(8,128)(2,1)}, u32[]{:S(2)}) copy-start(bf16[896,512]{1,0:T(8,128)(2,1)} %param.7) | copy-start | bytes 2752516
  0.0 75.9 %copy-start.1 = (bf16[512,896]{1,0:T(8,128)(2,1)S(1)}, bf16[512,896]{1,0:T(8,128)(2,1)}, u32[]{:S(2)}) copy-start(bf16[512,896]{1,0:T(8,128)(2,1)} %param.5) | copy-start | bytes 2752516
  0.0 77.6 %collective-permute-start = (bf16[512,896]{1,0:T(8,128)(2,1)}, bf16[512,896]{1,0:T(8,128)(2,1)S(1)}, u32[]{:S(2)}, u32[]{:S(2)}) collective-permute-start(bf16[512,896]{1,0:T(8,128)(2,1)} %param.5), channel_id=1, source_target_pairs={{0,1},{1,0},{2,3},{3,2},{4,5},{5,4},{6,7},{7,6},{8,9},{9,8},{10,11... | collective-permute-start | bytes 2752520 | tf_op jit(solution)/shard_map/ppermute | solution.py:17
  2.1 75.5 %collective-permute-start.1 = (bf16[512,896]{1,0:T(8,128)(2,1)}, bf16[512,896]{1,0:T(8,128)(2,1)}, u32[]{:S(2)}, u32[]{:S(2)}) collective-permute-start(bf16[512,896]{1,0:T(8,128)(2,1)} %param.6), channel_id=1, source_target_pairs={{0,1},{1,0},{2,3},{3,2},{4,5},{5,4},{6,7},{7,6},{8,9},{9,8},{10,11... | collective-permute-start | bytes 2752520 | tf_op jit(solution)/shard_map/ppermute | solution.py:17

commit v3 on v2

--- a/solution.py
+++ b/solution.py
@@ -22,8 +22,8 @@
     rows, features = tokens.shape
     mp, dp, guide = (lax.axis_size(axis) for axis in ("mp", "dp", "guide"))
     core = lax.axis_index("guide")
-    own_weights = jnp.concatenate([w_gate, w_up], axis=1)
-    other_weights = jnp.concatenate([from_other_core(w_gate), from_other_core(w_up)], axis=1)
+    own_weights = lax.optimization_barrier(jnp.concatenate([w_gate, w_up], axis=1))
+    other_weights = from_other_core(own_weights)
     blocks = lax.all_gather(tokens, ("mp", "guide"), axis=0, tiled=False)
     blocks = blocks.reshape(dp, guide, guide, rows, features)
     mine = lax.dynamic_index_in_dim(blocks, core, 1, keepdims=False)

time: 154 us -> 152 us (0.987)
  starting transfers between devices: 4.51 us -> 1.95 us
  other arithmetic: 0.79 us -> 2.46 us
    ppermute x2 -> x1, starting transfers between devices: 4.51 us -> 1.95 us  [from_other_core(): lax.ppermute(array, 'guide', [(core, (core + 1) % count) for core in rang...]
    concatenate x0 -> x1, other arithmetic: none -> 1.68 us  [per_device(): jnp.concatenate([w_gate, w_up], axis=1)]
  transfers between devices with their start and end apart: 2 -> 1, of which waited for: 0 -> 0; matrix products, arithmetic and copies ran while one was open for 1% -> 0% of each run, Pallas kernels for 0% -> 0%
where the time goes in v3:
time: 152 us; the launch traced here: 151 us
  blocking collectives  144 us (95%)
  matrix products  3.12 us (2%)
  other arithmetic  2.46 us (2%)
  starting transfers between devices  1.95 us (1%)
    all_gather x1, blocking collectives, per_device(): blocks = lax.all_gather(tokens, ('mp', 'guide'), axis=0, tiled=False)  71 us
    all_to_all x2, blocking collectives, summed_on_arrival(): lax.all_to_all(tiles, axis, split_axis=0, concat_axis=0, tiled=True)  55.9 us
    all_gather x1, blocking collectives, per_device(): hidden = lax.all_gather(hidden_share, ('dp', 'guide'), axis=0, tiled=True)  16.6 us
  transfers between devices with their start and end apart: 1, of which 0 were waited for; matrix products, arithmetic and copies ran while one was open for 0% of the time, Pallas kernels for 0%

profile of v3, /device:TPU:80, one launch (start us, length us, event | category | flops | bytes accessed | tf_op | source)
XLA Modules:
  0.0 151.2 jit_solution(9951680518774071853)
XLA Ops:
  0.0 0.0 copy-start
  0.0 0.0 copy-start.1
  0.0 1.7 %pad_maximum_fusion = bf16[512,1792]{1,0:T(8,128)(2,1)S(1)} fusion(bf16[512,896]{1,0:T(8,128)(2,1)} %param.6, bf16[512,896]{1,0:T(8,128)(2,1)} %param.5), kind=kLoop, calls=%fused_computation.2 | loop fusion | flops 3670016 | bytes 3670016 | tf_op jit(solution)/shard_map/concatenate | solution.py:25
  1.7 2.0 %collective-permute-start = (bf16[512,1792]{1,0:T(8,128)(2,1)S(1)}, bf16[512,1792]{1,0:T(8,128)(2,1)}, u32[]{:S(2)}, u32[]{:S(2)}) collective-permute-start(bf16[512,1792]{1,0:T(8,128)(2,1)S(1)} %pad_maximum_fusion), channel_id=1, source_target_pairs={{0,1},{1,0},{2,3},{3,2},{4,5},{5,4},{6,7},{7,6},{8,9},{9,8},{10,11... | collective-permute-start | bytes 5505032 | tf_op jit(solution)/shard_map/ppermute | solution.py:17
  3.7 0.0 copy-done.1
  3.7 71.0 %all-gather = bf16[768,512]{1,0:T(8,128)(2,1)S(1)} all-gather(bf16[24,512]{1,0:T(8,128)(2,1)S(1)} %copy-done.1), channel_id=2, replica_groups=mesh['groups'=2,'mp'=16,'dp'=8,'guide'=2] {'mp','guide'}, dimensions={0}, use_global_device_ids=true | all-gather | bytes 811008 | tf_op jit(solution)/shard_map/all_gather | solution.py:27
  74.7 0.5 fusion.3
  75.3 0.0 collective-permute-done
  75.3 2.0 %fusion = bf16[192,1792]{1,0:T(8,128)(2,1)S(1)} fusion(f32[192,1792]{1,0:T(8,128)S(1)} %fusion.3, bf16[192,512]{1,0:T(8,128)(2,1)S(1)} %bitcast.22, bf16[512,1792]{1,0:T(8,128)(2,1)} %collective-permute-done), kind=kOutput, calls=%fused_computation.1 | convolution fusion | flops 353009664 | bytes 4096000 | tf_op jit(solution)/shard_map/dot_general | solution.py:32
  77.3 28.6 %all_to_all.10 = bf16[8,24,1792]{2,1,0:T(8,128)(2,1)S(1)} all-to-all(bf16[8,24,1792]{2,1,0:T(8,128)(2,1)S(1)} %bitcast.20), channel_id=1, replica_groups=mesh['groups'=2,'mp'=16,'dp'=8,'guide'=2] {'dp'}, dimensions={0} | all-to-all | bytes 1376256 | tf_op jit(solution)/shard_map/all_to_all | solution.py:8
  105.9 0.1 add_bitcast_fusion
  106.1 16.6 %all_gather.11 = bf16[384,896]{1,0:T(8,128)(2,1)S(1)} all-gather(bf16[24,896]{1,0:T(8,128)(2,1)S(1)} %fusion.1), channel_id=1, replica_groups=mesh['groups'=2,'mp'=16,'dp'=8,'guide'=2] {'dp','guide'}, dimensions={0}, use_global_device_ids=true | all-gather | bytes 731136 | tf_op jit(solution)/shard_map/all_gather | solution.py:38
  122.7 0.0 copy-done
  122.7 0.6 convolution_convert_fusion
  123.3 27.3 %all_to_all.11 = bf16[16,24,512]{2,1,0:T(8,128)(2,1)S(1)} all-to-all(bf16[16,24,512]{2,1,0:T(8,128)(2,1)S(1)} %bitcast.24), channel_id=1, replica_groups=mesh['groups'=2,'mp'=16,'dp'=8,'guide'=2] {'mp'}, dimensions={0} | all-to-all | bytes 786432 | tf_op jit(solution)/shard_map/all_to_all | solution.py:8
  150.6 0.7 fusion.2
  (2 shorter events, 0.1 us)
Async XLA Ops:
  0.0 122.7 %copy-start = (bf16[896,512]{1,0:T(8,128)(2,1)S(1)}, bf16[896,512]{1,0:T(8,128)(2,1)}, u32[]{:S(2)}) copy-start(bf16[896,512]{1,0:T(8,128)(2,1)} %param.7) | copy-start | bytes 2752516
  0.0 3.7 %copy-start.1 = (bf16[24,512]{1,0:T(8,128)(2,1)S(1)}, bf16[24,512]{1,0:T(8,128)(2,1)}, u32[]{:S(2)}) copy-start(bf16[24,512]{1,0:T(8,128)(2,1)} %param.4) | copy-start | bytes 73732
  1.7 73.6 %collective-permute-start = (bf16[512,1792]{1,0:T(8,128)(2,1)S(1)}, bf16[512,1792]{1,0:T(8,128)(2,1)}, u32[]{:S(2)}, u32[]{:S(2)}) collective-permute-start(bf16[512,1792]{1,0:T(8,128)(2,1)S(1)} %pad_maximum_fusion), channel_id=1, source_target_pairs={{0,1},{1,0},{2,3},{3,2},{4,5},{5,4},{6,7},{7,6},{8,9},{9,8},{10,11... | collective-permute-start | bytes 5505032 | tf_op jit(solution)/shard_map/ppermute | solution.py:17

commit v4 on v3

--- a/solution.py
+++ b/solution.py
@@ -22,17 +22,19 @@
     rows, features = tokens.shape
     mp, dp, guide = (lax.axis_size(axis) for axis in ("mp", "dp", "guide"))
     core = lax.axis_index("guide")
-    own_weights = lax.optimization_barrier(jnp.concatenate([w_gate, w_up], axis=1))
-    other_weights = from_other_core(own_weights)
-    blocks = lax.all_gather(tokens, ("mp", "guide"), axis=0, tiled=False)
-    blocks = blocks.reshape(dp, guide, guide, rows, features)
-    mine = lax.dynamic_index_in_dim(blocks, core, 1, keepdims=False)
-    own = lax.dynamic_index_in_dim(mine, core, 1, keepdims=False).reshape(-1, features)
-    other = lax.dynamic_index_in_dim(mine, 1 - core, 1, keepdims=False).reshape(-1, features)
-    chip_terms = jnp.dot(own, own_weights, preferred_element_type=jnp.float32) + jnp.dot(
-        other, other_weights, preferred_element_type=jnp.float32
-    )
-    chip_terms = chip_terms.astype(jnp.bfloat16).reshape(dp, rows, -1)
+    paired_weights = jnp.concatenate([w_gate, w_up], axis=1)
+    blocks = lax.all_gather(tokens, "mp", axis=0, tiled=False)
+    blocks = blocks.reshape(dp, guide, rows, features)
+
+    def terms(owner):
+        owned = lax.dynamic_index_in_dim(blocks, owner, 1, keepdims=False)
+        return jnp.dot(
+            owned.reshape(-1, features), paired_weights, preferred_element_type=jnp.float32
+        )
+
+    received = from_other_core(terms(1 - core))
+    own = lax.optimization_barrier(terms(core))
+    chip_terms = (own + received).astype(jnp.bfloat16).reshape(dp, rows, -1)
     summed = summed_on_arrival(chip_terms, "dp")
     hidden_share = (jax.nn.silu(summed[:, :columns]) * summed[:, columns:]).astype(jnp.bfloat16)
     hidden = lax.all_gather(hidden_share, ("dp", "guide"), axis=0, tiled=True)

time: 152 us -> 153 us (level)
  local copies, waits for them, and re-layouts: 0.04 us -> 2.61 us
  waiting for transfers between devices: 0.01 us -> 2.56 us
  other arithmetic: 2.46 us -> 0.92 us
    ppermute x1, waiting for transfers between devices: 0.01 us -> 2.56 us  [from_other_core(): lax.ppermute(array, 'guide', [(core, (core + 1) % count) for core in rang...]
    concatenate x1 -> x0, other arithmetic: 1.68 us -> none  [per_device(): jnp.concatenate([w_gate, w_up], axis=1)]
  transfers between devices with their start and end apart: 1 -> 1, of which waited for: 0 -> 1; matrix products, arithmetic and copies ran while one was open for 0% -> 0% of each run, Pallas kernels for 0% -> 0%
where the time goes in v4:
time: 153 us
  blocking collectives  143 us (93%)
  local copies, waits for them, and re-layouts  2.61 us (2%)
  waiting for transfers between devices  2.56 us (2%)
  starting transfers between devices  1.95 us (1%)
  matrix products  1.62 us (1%)
    all_gather x1, blocking collectives, per_device(): blocks = lax.all_gather(tokens, 'mp', axis=0, tiled=False)  70.5 us
    all_to_all x2, blocking collectives, summed_on_arrival(): lax.all_to_all(tiles, axis, split_axis=0, concat_axis=0, tiled=True)  55.7 us
    all_gather x1, blocking collectives, per_device(): hidden = lax.all_gather(hidden_share, ('dp', 'guide'), axis=0, tiled=True)  16.6 us
  transfers between devices with their start and end apart: 1, of which 1 were waited for; matrix products, arithmetic and copies ran while one was open for 0% of the time, Pallas kernels for 0%

profile of v4, /device:TPU:80, one launch (start us, length us, event | category | flops | bytes accessed | tf_op | source)
XLA Modules:
  0.0 152.6 jit_solution(10927700330896320819)
XLA Ops:
  0.0 0.0 copy-start
  0.0 70.5 %all-gather = bf16[384,512]{1,0:T(8,128)(2,1)S(1)} all-gather(bf16[24,512]{1,0:T(8,128)(2,1)} %param.4), channel_id=2, replica_groups=mesh['groups'=2,'mp'=16,'dp'=8,'guide'=2] {'mp'}, dimensions={0}, use_global_device_ids=true | all-gather | bytes 417792 | tf_op jit(solution)/shard_map/all_gather | solution.py:26
  70.5 1.3 constant_dynamic-update-slice_fusion.1
  71.8 1.3 constant_dynamic-update-slice_fusion
  73.1 0.5 fusion.3
  73.7 2.0 %collective-permute-start = (f32[192,1792]{1,0:T(8,128)S(1)}, f32[192,1792]{1,0:T(8,128)S(1)}, u32[]{:S(2)}, u32[]{:S(2)}) collective-permute-start(f32[192,1792]{1,0:T(8,128)S(1)} %fusion.3), channel_id=1, source_target_pairs={{0,1},{1,0},{2,3},{3,2},{4,5},{5,4},{6,7},{7,6},{8,9},{9,8},{10,11... | collective-permute-start | bytes 4128776 | tf_op jit(solution)/shard_map/ppermute | solution.py:17
  75.6 0.5 fusion.2
  76.2 2.6 %collective-permute-done = f32[192,1792]{1,0:T(8,128)S(1)} collective-permute-done((f32[192,1792]{1,0:T(8,128)S(1)}, f32[192,1792]{1,0:T(8,128)S(1)}, u32[]{:S(2)}, u32[]{:S(2)}) %collective-permute-start) | collective-permute-done | bytes 1376288 | tf_op jit(solution)/shard_map/ppermute | solution.py:17
  78.7 0.1 add_convert_fusion
  78.9 28.4 %all_to_all.10 = bf16[8,24,1792]{2,1,0:T(8,128)(2,1)S(1)} all-to-all(bf16[8,24,1792]{2,1,0:T(8,128)(2,1)S(1)} %bitcast.20), channel_id=1, replica_groups=mesh['groups'=2,'mp'=16,'dp'=8,'guide'=2] {'dp'}, dimensions={0} | all-to-all | bytes 1376256 | tf_op jit(solution)/shard_map/all_to_all | solution.py:8
  107.3 0.1 add_bitcast_fusion
  107.4 16.6 %all_gather.11 = bf16[384,896]{1,0:T(8,128)(2,1)S(1)} all-gather(bf16[24,896]{1,0:T(8,128)(2,1)S(1)} %fusion), channel_id=1, replica_groups=mesh['groups'=2,'mp'=16,'dp'=8,'guide'=2] {'dp','guide'}, dimensions={0}, use_global_device_ids=true | all-gather | bytes 731136 | tf_op jit(solution)/shard_map/all_gather | solution.py:40
  124.1 0.0 copy-done
  124.1 0.6 convolution_convert_fusion
  124.6 27.3 %all_to_all.11 = bf16[16,24,512]{2,1,0:T(8,128)(2,1)S(1)} all-to-all(bf16[16,24,512]{2,1,0:T(8,128)(2,1)S(1)} %bitcast.24), channel_id=1, replica_groups=mesh['groups'=2,'mp'=16,'dp'=8,'guide'=2] {'mp'}, dimensions={0} | all-to-all | bytes 786432 | tf_op jit(solution)/shard_map/all_to_all | solution.py:8
  151.9 0.7 fusion.1
  (2 shorter events, 0.1 us)
Async XLA Ops:
  0.0 124.1 %copy-start = (bf16[896,512]{1,0:T(8,128)(2,1)S(1)}, bf16[896,512]{1,0:T(8,128)(2,1)}, u32[]{:S(2)}) copy-start(bf16[896,512]{1,0:T(8,128)(2,1)} %param.7) | copy-start | bytes 2752516
  73.7 5.1 %collective-permute-start = (f32[192,1792]{1,0:T(8,128)S(1)}, f32[192,1792]{1,0:T(8,128)S(1)}, u32[]{:S(2)}, u32[]{:S(2)}) collective-permute-start(f32[192,1792]{1,0:T(8,128)S(1)} %fusion.3), channel_id=1, source_target_pairs={{0,1},{1,0},{2,3},{3,2},{4,5},{5,4},{6,7},{7,6},{8,9},{9,8},{10,11... | collective-permute-start | bytes 4128776 | tf_op jit(solution)/shard_map/ppermute | solution.py:17

commit v5 on v4

--- a/solution.py
+++ b/solution.py
@@ -22,14 +22,13 @@
     rows, features = tokens.shape
     mp, dp, guide = (lax.axis_size(axis) for axis in ("mp", "dp", "guide"))
     core = lax.axis_index("guide")
-    paired_weights = jnp.concatenate([w_gate, w_up], axis=1)
     blocks = lax.all_gather(tokens, "mp", axis=0, tiled=False)
     blocks = blocks.reshape(dp, guide, rows, features)
 
     def terms(owner):
-        owned = lax.dynamic_index_in_dim(blocks, owner, 1, keepdims=False)
-        return jnp.dot(
-            owned.reshape(-1, features), paired_weights, preferred_element_type=jnp.float32
+        owned = lax.dynamic_index_in_dim(blocks, owner, 1, keepdims=False).reshape(-1, features)
+        return jnp.concatenate(
+            [jnp.dot(owned, w, preferred_element_type=jnp.float32) for w in (w_gate, w_up)], axis=1
         )
 
     received = from_other_core(terms(1 - core))

time: 153 us -> 151 us (0.987)
  local copies, waits for them, and re-layouts: 2.61 us -> 0.79 us
  transfers between devices with their start and end apart: 1 -> 1, of which waited for: 1 -> 1; matrix products, arithmetic and copies ran while one was open for 0% -> 1% of each run, Pallas kernels for 0% -> 0%
where the time goes in v5:
time: 151 us
  blocking collectives  143 us (95%)
  waiting for transfers between devices  2.21 us (1%)
  matrix products  2.12 us (1%)
  starting transfers between devices  1.95 us (1%)
    all_gather x1, blocking collectives, per_device(): blocks = lax.all_gather(tokens, 'mp', axis=0, tiled=False)  70.5 us
    all_to_all x2, blocking collectives, summed_on_arrival(): lax.all_to_all(tiles, axis, split_axis=0, concat_axis=0, tiled=True)  55.8 us
    all_gather x1, blocking collectives, per_device(): hidden = lax.all_gather(hidden_share, ('dp', 'guide'), axis=0, tiled=True)  16.6 us
  transfers between devices with their start and end apart: 1, of which 1 were waited for; matrix products, arithmetic and copies ran while one was open for 1% of the time, Pallas kernels for 0%

profile of v5, /device:TPU:80, one launch (start us, length us, event | category | flops | bytes accessed | tf_op | source)
XLA Modules:
  0.0 151.2 jit_solution(467243203883209130)
XLA Ops:
  0.0 0.0 copy-start
  0.0 70.5 %all-gather = bf16[384,512]{1,0:T(8,128)(2,1)S(1)} all-gather(bf16[24,512]{1,0:T(8,128)(2,1)} %param.4), channel_id=2, replica_groups=mesh['groups'=2,'mp'=16,'dp'=8,'guide'=2] {'mp'}, dimensions={0}, use_global_device_ids=true | all-gather | bytes 417792 | tf_op jit(solution)/shard_map/all_gather | solution.py:25
  70.5 0.0 copy-start.1
  70.6 0.0 copy-done
  70.6 0.4 fusion.4
  71.0 0.7 copy-done.1
  71.7 0.4 fusion.5
  72.1 0.1 pad_maximum_fusion.1
  72.2 2.0 %collective-permute-start = (f32[192,1792]{1,0:T(8,128)S(1)}, f32[192,1792]{1,0:T(8,128)S(1)}, u32[]{:S(2)}, u32[]{:S(2)}) collective-permute-start(f32[192,1792]{1,0:T(8,128)S(1)} %pad_maximum_fusion.1), channel_id=1, source_target_pairs={{0,1},{1,0},{2,3},{3,2},{4,5},{5,4},{6,7},{7,6},{8,9},{9,8},{10,11... | collective-permute-start | bytes 4128776 | tf_op jit(solution)/shard_map/ppermute | solution.py:17
  74.2 0.4 fusion.2
  74.5 0.4 fusion.3
  74.9 0.1 pad_maximum_fusion
  75.0 2.2 %collective-permute-done = f32[192,1792]{1,0:T(8,128)S(1)} collective-permute-done((f32[192,1792]{1,0:T(8,128)S(1)}, f32[192,1792]{1,0:T(8,128)S(1)}, u32[]{:S(2)}, u32[]{:S(2)}) %collective-permute-start) | collective-permute-done | bytes 1376288 | tf_op jit(solution)/shard_map/ppermute | solution.py:17
  77.3 0.1 add_convert_fusion
  77.4 0.0 copy-start.2
  77.4 28.5 %all_to_all.10 = bf16[8,24,1792]{2,1,0:T(8,128)(2,1)S(1)} all-to-all(bf16[8,24,1792]{2,1,0:T(8,128)(2,1)S(1)} %bitcast.24), channel_id=1, replica_groups=mesh['groups'=2,'mp'=16,'dp'=8,'guide'=2] {'dp'}, dimensions={0} | all-to-all | bytes 1376256 | tf_op jit(solution)/shard_map/all_to_all | solution.py:8
  105.9 0.1 add_bitcast_fusion
  106.1 16.6 %all_gather.11 = bf16[384,896]{1,0:T(8,128)(2,1)S(1)} all-gather(bf16[24,896]{1,0:T(8,128)(2,1)S(1)} %fusion), channel_id=1, replica_groups=mesh['groups'=2,'mp'=16,'dp'=8,'guide'=2] {'dp','guide'}, dimensions={0}, use_global_device_ids=true | all-gather | bytes 731136 | tf_op jit(solution)/shard_map/all_gather | solution.py:39
  122.7 0.0 copy-done.2
  122.7 0.6 convolution_convert_fusion
  123.3 27.3 %all_to_all.11 = bf16[16,24,512]{2,1,0:T(8,128)(2,1)S(1)} all-to-all(bf16[16,24,512]{2,1,0:T(8,128)(2,1)S(1)} %bitcast.30), channel_id=1, replica_groups=mesh['groups'=2,'mp'=16,'dp'=8,'guide'=2] {'mp'}, dimensions={0} | all-to-all | bytes 786432 | tf_op jit(solution)/shard_map/all_to_all | solution.py:8
  150.6 0.7 fusion.1
  (2 shorter events, 0.1 us)
Async XLA Ops:
  0.0 70.6 %copy-start = (bf16[512,896]{1,0:T(8,128)(2,1)S(1)}, bf16[512,896]{1,0:T(8,128)(2,1)}, u32[]{:S(2)}) copy-start(bf16[512,896]{1,0:T(8,128)(2,1)} %param.5) | copy-start | bytes 2752516
  70.5 1.2 copy-start.1
  72.2 5.1 %collective-permute-start = (f32[192,1792]{1,0:T(8,128)S(1)}, f32[192,1792]{1,0:T(8,128)S(1)}, u32[]{:S(2)}, u32[]{:S(2)}) collective-permute-start(f32[192,1792]{1,0:T(8,128)S(1)} %pad_maximum_fusion.1), channel_id=1, source_target_pairs={{0,1},{1,0},{2,3},{3,2},{4,5},{5,4},{6,7},{7,6},{8,9},{9,8},{10,11... | collective-permute-start | bytes 4128776 | tf_op jit(solution)/shard_map/ppermute | solution.py:17
  77.4 45.3 %copy-start.2 = (bf16[896,512]{1,0:T(8,128)(2,1)S(1)}, bf16[896,512]{1,0:T(8,128)(2,1)}, u32[]{:S(2)}) copy-start(bf16[896,512]{1,0:T(8,128)(2,1)} %param.7) | copy-start | bytes 2752516

commit v6 on v3

--- a/solution.py
+++ b/solution.py
@@ -22,22 +22,37 @@
     rows, features = tokens.shape
     mp, dp, guide = (lax.axis_size(axis) for axis in ("mp", "dp", "guide"))
     core = lax.axis_index("guide")
+    head = 2 * rows // 3
+    tail = rows - head
+    own_parity = lax.axis_index("mp") % guide == core
+    other_tokens = from_other_core(tokens)
+    both = jnp.stack([tokens, other_tokens])
     own_weights = lax.optimization_barrier(jnp.concatenate([w_gate, w_up], axis=1))
     other_weights = from_other_core(own_weights)
-    blocks = lax.all_gather(tokens, ("mp", "guide"), axis=0, tiled=False)
-    blocks = blocks.reshape(dp, guide, guide, rows, features)
-    mine = lax.dynamic_index_in_dim(blocks, core, 1, keepdims=False)
-    own = lax.dynamic_index_in_dim(mine, core, 1, keepdims=False).reshape(-1, features)
-    other = lax.dynamic_index_in_dim(mine, 1 - core, 1, keepdims=False).reshape(-1, features)
-    chip_terms = jnp.dot(own, own_weights, preferred_element_type=jnp.float32) + jnp.dot(
-        other, other_weights, preferred_element_type=jnp.float32
+    owned = jnp.where(
+        own_parity,
+        both[:, :head],
+        jnp.pad(both[:, head:], ((0, 0), (0, head - tail), (0, 0))),
     )
-    chip_terms = chip_terms.astype(jnp.bfloat16).reshape(dp, rows, -1)
-    summed = summed_on_arrival(chip_terms, "dp")
+    blocks = lax.all_gather(owned.reshape(-1, features), "mp", axis=0, tiled=True)
+    blocks = blocks.reshape(dp, guide, 2, head, features)
+    heads = lax.dynamic_index_in_dim(blocks, core, 1, keepdims=False)
+    tails = lax.dynamic_index_in_dim(blocks, 1 - core, 1, keepdims=False)[:, :, :tail]
+    mine = jnp.concatenate([heads, tails], axis=2)
+    chip_terms = jnp.dot(
+        mine[:, 0].reshape(-1, features), own_weights, preferred_element_type=jnp.float32
+    ) + jnp.dot(
+        mine[:, 1].reshape(-1, features), other_weights, preferred_element_type=jnp.float32
+    )
+    summed = summed_on_arrival(chip_terms.astype(jnp.bfloat16).reshape(dp, rows, -1), "dp")
     hidden_share = (jax.nn.silu(summed[:, :columns]) * summed[:, columns:]).astype(jnp.bfloat16)
     hidden = lax.all_gather(hidden_share, ("dp", "guide"), axis=0, tiled=True)
     output_terms = jnp.dot(hidden, w_down, preferred_element_type=jnp.float32).astype(jnp.bfloat16)
-    return summed_on_arrival(output_terms.reshape(mp, rows, -1), "mp").astype(jnp.bfloat16)
+    output_terms = output_terms.reshape(dp, guide, rows, -1)
+    placed = jnp.concatenate(
+        [output_terms[:, :, :head], output_terms[:, ::-1, head:]], axis=2
+    )
+    return summed_on_arrival(placed.reshape(mp, rows, -1), "mp").astype(jnp.bfloat16)
 
 
 def solution(mesh):

time: 152 us -> 149 us (0.980)
  blocking collectives: 144 us -> 137 us
  starting transfers between devices: 1.95 us -> 4.39 us
    all_to_all x2, blocking collectives: 55.9 us -> 50.1 us  [summed_on_arrival(): lax.all_to_all(tiles, axis, split_axis=0, concat_axis=0, tiled=True)]
    ppermute x1 -> x2, starting transfers between devices: 1.95 us -> 4.39 us  [from_other_core(): lax.ppermute(array, 'guide', [(core, (core + 1) % count) for core in rang...]
  transfers between devices with their start and end apart: 1 -> 2, of which waited for: 0 -> 1; matrix products, arithmetic and copies ran while one was open for 0% -> 0% of each run, Pallas kernels for 0% -> 0%
where the time goes in v6:
time: 149 us
  blocking collectives  137 us (92%)
  starting transfers between devices  4.39 us (3%)
  matrix products  3.13 us (2%)
  other arithmetic  2.53 us (2%)
    all_gather x1, blocking collectives, per_device(): lax.all_gather(owned.reshape(-1, features), 'mp', axis=0, tiled=True)  70.8 us
    all_to_all x2, blocking collectives, summed_on_arrival(): lax.all_to_all(tiles, axis, split_axis=0, concat_axis=0, tiled=True)  50.1 us
    all_gather x1, blocking collectives, per_device(): hidden = lax.all_gather(hidden_share, ('dp', 'guide'), axis=0, tiled=True)  16.4 us
    ppermute x2, starting transfers between devices, from_other_core(): lax.ppermute(array, 'guide', [(core, (core + 1) % count) for core in rang...  4.39 us
  transfers between devices with their start and end apart: 2, of which 1 were waited for; matrix products, arithmetic and copies ran while one was open for 0% of the time, Pallas kernels for 0%

profile of v6, /device:TPU:80, one launch (start us, length us, event | category | flops | bytes accessed | tf_op | source)
XLA Modules:
  0.0 149.1 jit_solution(11184921918008794010)
XLA Ops:
  0.0 0.0 copy-start
  0.0 0.0 copy-start.1
  0.0 1.7 %pad_maximum_fusion = bf16[512,1792]{1,0:T(8,128)(2,1)S(1)} fusion(bf16[512,896]{1,0:T(8,128)(2,1)} %param.6, bf16[512,896]{1,0:T(8,128)(2,1)} %param.5), kind=kLoop, calls=%fused_computation.2 | loop fusion | flops 3670016 | bytes 3670016 | tf_op jit(solution)/shard_map/concatenate | solution.py:30
  1.7 2.0 %collective-permute-start.1 = (bf16[512,1792]{1,0:T(8,128)(2,1)S(1)}, bf16[512,1792]{1,0:T(8,128)(2,1)}, u32[]{:S(2)}, u32[]{:S(2)}) collective-permute-start(bf16[512,1792]{1,0:T(8,128)(2,1)S(1)} %pad_maximum_fusion), channel_id=1, source_target_pairs={{0,1},{1,0},{2,3},{3,2},{4,5},{5,4},{6,7},{7,6},{8,9},{9,8},{10,11... | collective-permute-start | bytes 5505032 | tf_op jit(solution)/shard_map/ppermute | solution.py:17
  3.6 0.0 copy-done.1
  3.7 2.4 %collective-permute-start = (bf16[24,512]{1,0:T(8,128)(2,1)S(1)}, bf16[24,512]{1,0:T(8,128)(2,1)S(1)}, u32[]{:S(2)}, u32[]{:S(2)}) collective-permute-start(bf16[24,512]{1,0:T(8,128)(2,1)S(1)} %copy-done.1), channel_id=1, source_target_pairs={{0,1},{1,0},{2,3},{3,2},{4,5},{5,4},{6,7},{7,6},{8,9},{9,8},{10,11... | collective-permute-start | bytes 73736 | tf_op jit(solution)/shard_map/ppermute | solution.py:17
  6.1 1.4 collective-permute-done
  7.5 70.8 %all_gather.6 = bf16[512,512]{1,0:T(8,128)(2,1)S(1)} all-gather(bf16[32,512]{1,0:T(8,128)(2,1)S(1)} %bitcast.35), channel_id=1, replica_groups=mesh['groups'=2,'mp'=16,'dp'=8,'guide'=2] {'mp'}, dimensions={0}, use_global_device_ids=true | all-gather | bytes 557056 | tf_op jit(solution)/shard_map/all_gather | solution.py:37
  78.5 0.5 fusion.9
  79.0 0.0 collective-permute-done.1
  79.0 2.0 %fusion = bf16[192,1792]{1,0:T(8,128)(2,1)S(1)} fusion(f32[192,1792]{1,0:T(8,128)S(1)} %fusion.9, bf16[192,512]{1,0:T(8,128)(2,1)S(1)} %bitcast.31, bf16[512,1792]{1,0:T(8,128)(2,1)} %collective-permute-done.1), kind=kOutput, calls=%fused_computation.1 | convolution fusion | flops 353009664 | bytes 4096000 | tf_op jit(solution)/shard_map/dot_general | solution.py:44
  81.1 22.2 %all_to_all.10 = bf16[8,24,1792]{2,1,0:T(8,128)(2,1)S(1)} all-to-all(bf16[8,24,1792]{2,1,0:T(8,128)(2,1)S(1)} %bitcast.28), channel_id=1, replica_groups=mesh['groups'=2,'mp'=16,'dp'=8,'guide'=2] {'dp'}, dimensions={0} | all-to-all | bytes 1376256 | tf_op jit(solution)/shard_map/all_to_all | solution.py:8
  103.2 0.1 add_bitcast_fusion
  103.4 16.4 %all_gather.7 = bf16[384,896]{1,0:T(8,128)(2,1)S(1)} all-gather(bf16[24,896]{1,0:T(8,128)(2,1)S(1)} %fusion.2), channel_id=1, replica_groups=mesh['groups'=2,'mp'=16,'dp'=8,'guide'=2] {'dp','guide'}, dimensions={0}, use_global_device_ids=true | all-gather | bytes 731136 | tf_op jit(solution)/shard_map/all_gather | solution.py:49
  119.8 0.0 copy-done
  119.8 0.6 convolution_convert_fusion
  120.5 28.0 %all_to_all.11 = bf16[16,24,512]{2,1,0:T(8,128)(2,1)S(1)} all-to-all(bf16[16,24,512]{2,1,0:T(8,128)(2,1)S(1)} %bitcast.30), channel_id=1, replica_groups=mesh['groups'=2,'mp'=16,'dp'=8,'guide'=2] {'mp'}, dimensions={0} | all-to-all | bytes 786432 | tf_op jit(solution)/shard_map/all_to_all | solution.py:8
  148.4 0.7 fusion.5
  (9 shorter events, 0.2 us)
Async XLA Ops:
  0.0 119.8 %copy-start = (bf16[896,512]{1,0:T(8,128)(2,1)S(1)}, bf16[896,512]{1,0:T(8,128)(2,1)}, u32[]{:S(2)}) copy-start(bf16[896,512]{1,0:T(8,128)(2,1)} %param.7) | copy-start | bytes 2752516
  0.0 3.6 %copy-start.1 = (bf16[24,512]{1,0:T(8,128)(2,1)S(1)}, bf16[24,512]{1,0:T(8,128)(2,1)}, u32[]{:S(2)}) copy-start(bf16[24,512]{1,0:T(8,128)(2,1)} %param.4) | copy-start | bytes 73732
  1.7 77.3 %collective-permute-start.1 = (bf16[512,1792]{1,0:T(8,128)(2,1)S(1)}, bf16[512,1792]{1,0:T(8,128)(2,1)}, u32[]{:S(2)}, u32[]{:S(2)}) collective-permute-start(bf16[512,1792]{1,0:T(8,128)(2,1)S(1)} %pad_maximum_fusion), channel_id=1, source_target_pairs={{0,1},{1,0},{2,3},{3,2},{4,5},{5,4},{6,7},{7,6},{8,9},{9,8},{10,11... | collective-permute-start | bytes 5505032 | tf_op jit(solution)/shard_map/ppermute | solution.py:17
  3.7 3.9 %collective-permute-start = (bf16[24,512]{1,0:T(8,128)(2,1)S(1)}, bf16[24,512]{1,0:T(8,128)(2,1)S(1)}, u32[]{:S(2)}, u32[]{:S(2)}) collective-permute-start(bf16[24,512]{1,0:T(8,128)(2,1)S(1)} %copy-done.1), channel_id=1, source_target_pairs={{0,1},{1,0},{2,3},{3,2},{4,5},{5,4},{6,7},{7,6},{8,9},{9,8},{10,11... | collective-permute-start | bytes 73736 | tf_op jit(solution)/shard_map/ppermute | solution.py:17
